TPU v7x, 8 devices: a whole 2x2x1 slice. The times are simulated.
8 devices in a mesh: pod: 1 (over z), data: 2 (over y), expert: 4 (over x, core).
Axes of the slice: x: 2, y: 2, z: 1, core: 2. Of those that a mesh axis runs over, the one named last changes fastest.
Arguments:
- tokens: bfloat16 [16384, 1024], P(('pod', 'data', 'expert'))
- routes: int32 [16384, 8], P(('pod', 'data', 'expert'))
- gates: float32 [16384, 8], P(('pod', 'data', 'expert'))
- grad_y: bfloat16 [16384, 1024], P(('pod', 'data', 'expert'))
- w_in1: bfloat16 [32, 1024, 512], P('expert')
- w_in3: bfloat16 [32, 1024, 512], P('expert')
- w_out: bfloat16 [32, 512, 1024], P('expert')
Outputs:
- output 1: bfloat16 [16384, 1024], P(('pod', 'data', 'expert'))
- output 2: bfloat16 [16384, 1024], P(('pod', 'data', 'expert'))
- output 3: float32 [32, 1024, 512], P(('pod', 'expert'))
- output 4: float32 [32, 1024, 512], P(('pod', 'expert'))
- output 5: float32 [32, 512, 1024], P(('pod', 'expert'))
All inputs are finite; a program needn't handle non-finite values.
Results may differ from a plain program's by a relative error of at most 0.0102961.
Values are sent between devices in bfloat16 or wider.
A program may use at most 1 GiB of HBM per device.

v0:
```python
import jax
import jax.numpy as jnp
from jax import lax
from jax.sharding import PartitionSpec as P

N_HOT = 2


def value_a10(tok_dev, top_k, n_exp):
    cap_hot = 3 * tok_dev // 8
    cap_cold = max(8, ((tok_dev * top_k - N_HOT * cap_hot) // (n_exp - N_HOT) + 7) // 8 * 8)
    return cap_cold, cap_hot


def route_rows(routes_dev, n_exp, cap_cold, cap_hot):
    flat_exp = routes_dev.reshape(-1)
    n_slots = flat_exp.shape[0]
    order = jnp.argsort(flat_exp, stable=True)
    counts = jax.ops.segment_sum(jnp.ones((n_slots,), jnp.int32), flat_exp, num_segments=n_exp)
    starts = jnp.cumsum(counts) - counts
    rank_sorted = jnp.arange(n_slots, dtype=jnp.int32) - starts[flat_exp[order]]
    slot_rank = jnp.zeros((n_slots,), jnp.int32).at[order].set(rank_sorted)
    hot_index = jnp.where(flat_exp == 0, 0, jnp.where(flat_exp == n_exp // 2, 1, -1))
    cold_row = jnp.where((hot_index < 0) & (slot_rank < cap_cold), flat_exp * cap_cold + slot_rank, n_exp * cap_cold)
    hot_row = jnp.where(hot_index >= 0, hot_index * cap_hot + slot_rank, N_HOT * cap_hot)
    return cold_row, hot_row


def gather_rows(slot_rows, x_local, dy_local, gate_flat, n_rows):
    n_slots = slot_rows.shape[0]
    tok_n = x_local.shape[0]
    top_k = n_slots // tok_n
    src_tok = jnp.full((n_rows,), tok_n, jnp.int32).at[slot_rows].set(
        jnp.arange(n_slots, dtype=jnp.int32) // top_k, mode='drop')
    src_gate = jnp.zeros((n_rows,), jnp.float32).at[slot_rows].set(gate_flat, mode='drop')
    x_rows = jnp.take(x_local, src_tok, axis=0, mode='fill', fill_value=0)
    dy_rows = jnp.take(dy_local, src_tok, axis=0, mode='fill', fill_value=0)
    do_rows = (dy_rows.astype(jnp.float32) * src_gate[:, None]).astype(jnp.bfloat16)
    return x_rows, do_rows


def expert_fwd(x_rows, w_a, w_b, w_c):
    pre_a = jnp.einsum('esd,edf->esf', x_rows, w_a, preferred_element_type=jnp.float32).astype(jnp.bfloat16)
    pre_b = jnp.einsum('esd,edf->esf', x_rows, w_b, preferred_element_type=jnp.float32).astype(jnp.bfloat16)
    act_a = pre_a.astype(jnp.float32)
    hidden = (act_a * jax.nn.sigmoid(act_a) * pre_b.astype(jnp.float32)).astype(jnp.bfloat16)
    outs = jnp.einsum('esf,efd->esd', hidden, w_c, preferred_element_type=jnp.float32).astype(jnp.bfloat16)
    return outs, pre_a, pre_b, hidden


def expert_bwd(x_rows, do_rows, pre_a, pre_b, hidden, w_a, w_b, w_c):
    d_hidden = jnp.einsum('esd,efd->esf', do_rows, w_c, preferred_element_type=jnp.float32)
    act_a = pre_a.astype(jnp.float32)
    act_b = pre_b.astype(jnp.float32)
    sigma_a = jax.nn.sigmoid(act_a)
    d_pre_b = (d_hidden * act_a * sigma_a).astype(jnp.bfloat16)
    d_pre_a = (d_hidden * act_b * sigma_a * (1.0 + act_a * (1.0 - sigma_a))).astype(jnp.bfloat16)
    d_rows = (jnp.einsum('esf,edf->esd', d_pre_a, w_a, preferred_element_type=jnp.float32)
              + jnp.einsum('esf,edf->esd', d_pre_b, w_b, preferred_element_type=jnp.float32)).astype(jnp.bfloat16)
    grad_a = jnp.einsum('esd,esf->edf', x_rows, d_pre_a, preferred_element_type=jnp.float32)
    grad_b = jnp.einsum('esd,esf->edf', x_rows, d_pre_b, preferred_element_type=jnp.float32)
    grad_c = jnp.einsum('esf,esd->efd', hidden, do_rows, preferred_element_type=jnp.float32)
    return d_rows, grad_a, grad_b, grad_c


def combine(cold_rows, hot_rows, cold_vals, hot_vals, weights, tok_n):
    slot_vals = (jnp.take(cold_vals, cold_rows, axis=0, mode='fill', fill_value=0)
                 + jnp.take(hot_vals, hot_rows, axis=0, mode='fill', fill_value=0))
    slot_vals = slot_vals.reshape(tok_n, -1, cold_vals.shape[1]).astype(jnp.float32)
    if weights is not None:
        slot_vals = slot_vals * weights[:, :, None]
    return jnp.sum(slot_vals, axis=1).astype(jnp.bfloat16)


def solution(mesh):
    n_dev = mesh.shape['expert']
    row_spec = P(('pod', 'data', 'expert'), None)
    w_spec = P('expert', None, None)
    grad_spec = P(('pod', 'expert'), None, None)

    def body(tokens, routes, gates, grad_y, w_in1, w_in3, w_out):
        tok_n, d_model = tokens.shape
        top_k = routes.shape[1]
        exp_local = w_in1.shape[0]
        n_exp = exp_local * n_dev
        my_index = lax.axis_index('expert')
        cap_cold, cap_hot = value_a10(tok_n, top_k, n_exp)
        cold_rows, hot_rows = route_rows(routes, n_exp, cap_cold, cap_hot)
        gate_flat = gates.reshape(-1)
        cold_x, cold_do = gather_rows(cold_rows, tokens, grad_y, gate_flat, n_exp * cap_cold)
        hot_x, hot_do = gather_rows(hot_rows, tokens, grad_y, gate_flat, N_HOT * cap_hot)
        hot_x = hot_x.reshape(N_HOT, cap_hot, d_model)
        hot_do = hot_do.reshape(N_HOT, cap_hot, d_model)
        hot_local = [0, (n_exp // 2) % exp_local]
        hot_owner = [0, (n_exp // 2) // exp_local]

        def owned_copy(w_local):
            return jnp.stack([jnp.where(my_index == owner_idx, w_local[local_idx], 0)
                              for local_idx, owner_idx in zip(hot_local, hot_owner)])

        hot_w1, hot_w3, hot_w2 = lax.psum((owned_copy(w_in1), owned_copy(w_in3), owned_copy(w_out)), 'expert')

        recv_x = lax.all_to_all(cold_x.reshape(n_exp, cap_cold, d_model), 'expert', 0, 1, tiled=True)
        cold_out, cold_pre_a, cold_pre_b, cold_hidden = expert_fwd(recv_x, w_in1, w_in3, w_out)
        back_out = lax.all_to_all(cold_out, 'expert', 1, 0, tiled=True)
        hot_out, hot_pre_a, hot_pre_b, hot_hidden = expert_fwd(hot_x, hot_w1, hot_w3, hot_w2)
        y_out = combine(cold_rows, hot_rows, back_out.reshape(-1, d_model), hot_out.reshape(-1, d_model), gates, tok_n)

        recv_do = lax.all_to_all(cold_do.reshape(n_exp, cap_cold, d_model), 'expert', 0, 1, tiled=True)
        cold_dx, grad_w1, grad_w3, grad_w2 = expert_bwd(recv_x, recv_do, cold_pre_a, cold_pre_b, cold_hidden, w_in1, w_in3, w_out)
        back_dx = lax.all_to_all(cold_dx, 'expert', 1, 0, tiled=True)
        hot_dx, part_w1, part_w3, part_w2 = expert_bwd(hot_x, hot_do, hot_pre_a, hot_pre_b, hot_hidden, hot_w1, hot_w3, hot_w2)
        grad_x = combine(cold_rows, hot_rows, back_dx.reshape(-1, d_model), hot_dx.reshape(-1, d_model), None, tok_n)
        part_w1, part_w3, part_w2 = lax.psum((part_w1, part_w3, part_w2), 'expert')

        def add_owned(grad_local, hot_sum):
            for slot_h in range(N_HOT):
                grad_local = grad_local.at[hot_local[slot_h]].add(
                    jnp.where(my_index == hot_owner[slot_h], hot_sum[slot_h], 0.0))
            return grad_local

        grad_w1 = add_owned(grad_w1, part_w1)
        grad_w3 = add_owned(grad_w3, part_w3)
        grad_w2 = add_owned(grad_w2, part_w2)
        grad_w1, grad_w3, grad_w2 = lax.psum((grad_w1, grad_w3, grad_w2), 'data')
        return y_out, grad_x, grad_w1, grad_w3, grad_w2

    return jax.shard_map(body, mesh=mesh,
                         in_specs=(row_spec, row_spec, row_spec, row_spec, w_spec, w_spec, w_spec),
                         out_specs=(row_spec, row_spec, grad_spec, grad_spec, grad_spec),
                         check_vma=False)
```

profile of v0, /device:TPU:5, one launch (start us, length us, event | category | flops | bytes accessed | tf_op | source)
XLA Modules:
  0.0 3275.4 jit_solution(7144266925647895383)
XLA Ops:
  8.9 113.4 %scatter_custom_fusion = s32[32]{0:T(128)S(1)} fusion(s32[16384]{0:T(1024)S(1)} %reshape.276, s32[16384]{0:T(1024)S(1)} %broadcast_in_dim.111, s32[]{:T(128)} %constant.213.clone.1), kind=kCustom, calls=%fused_computation.161 | custom fusion | flops 16384 | bytes 132 | tf_op jit(solution)/shard_map/scatter-add | solution.py:19
  131.8 91.1 %gather_fusion = s32[16384]{0:T(1024)S(1)} fusion(s32[16384]{0:T(1024)S(1)} %reshape.276, s32[16384]{0:T(1024)S(1)} %get-tuple-element.133), kind=kCustom, calls=%fused_computation.8 | custom fusion | bytes 196608 | tf_op jit(solution)/shard_map/gather | solution.py:21
  232.5 15.9 select_subtract_fusion
  248.4 60.3 %scatter_custom_fusion.1 = s32[16384]{0:T(1024)S(1)} fusion(s32[16384]{0:T(1024)S(1)} %get-tuple-element.134, s32[16384]{0:T(1024)S(1)} %select_subtract_fusion, s32[]{:T(128)} %constant.213.clone.1), kind=kCustom, calls=%fused_computation.149 | custom fusion | bytes 65540 | tf_op jit(solution)/shard_map/scatter | solution.py:22
  309.5 60.3 %scatter_custom_fusion.2 = s32[15872]{0:T(1024)S(1)} fusion(s32[16384]{0:T(1024)S(1)} %get-tuple-element.118, s32[16384]{0:T(1024)S(1)} %add_select_fusion, s32[]{:T(128)} %constant.212.clone.1), kind=kCustom, calls=%fused_computation.152 | custom fusion | bytes 63492 | tf_op jit(solution)/shard_map/scatter | solution.py:33
  369.9 70.8 %gather_fusion.1 = bf16[15872,1024]{1,0:T(8,128)(2,1)} fusion(bf16[2048,1024]{1,0:T(8,128)(2,1)} %param.27, s32[16384]{0:T(1024)S(1)} %pad_clamp_fusion), kind=kCustom, calls=%fused_computation.clone | custom fusion | bytes 65075200 | tf_op jit(solution)/shard_map/jit(_take)/gather | solution.py:36
  440.7 22.5 broadcast_select_fusion
  463.2 10.3 all-to-all-start
  473.6 70.8 %gather_fusion.5 = bf16[15872,1024]{1,0:T(8,128)(2,1)} fusion(bf16[2048,1024]{1,0:T(8,128)(2,1)} %param.30, s32[16384]{0:T(1024)S(1)} %pad_clamp_fusion), kind=kCustom, calls=%fused_computation.4.clone | custom fusion | bytes 65075200 | tf_op jit(solution)/shard_map/jit(_take)/gather | solution.py:37
  545.3 60.5 %scatter_custom_fusion.4 = f32[15872]{0:T(1024)S(1)} fusion(s32[16384]{0:T(1024)} %copy-done.11, f32[16384]{0:T(1024)S(1)} %reshape.445, f32[]{:T(128)} %constant.229.clone.1), kind=kCustom, calls=%fused_computation.146 | custom fusion | bytes 64000 | tf_op jit(solution)/shard_map/scatter | solution.py:35
  605.8 22.2 multiply_convert_fusion
  628.1 195.9 %all-to-all-done = bf16[32,496,1024]{2,1,0:T(8,128)(2,1)} async-done(((bf16[32,496,1024]{2,1,0:T(8,128)(2,1)}), bf16[32,496,1024]{2,1,0:T(8,128)(2,1)}, u32[]{:S(2)}, u32[]{:S(2)}) %all-to-all-start) | async-done | bytes 32505888 | tf_op jit(solution)/shard_map/all_to_all | solution.py:103
  823.9 10.4 all-to-all-start.2
  843.0 60.4 %scatter_custom_fusion.3 = s32[1536]{0:T(1024)S(1)} fusion(s32[16384]{0:T(1024)} %get-tuple-element.132, s32[16384]{0:T(1024)} %copy-done.17, s32[]{:T(128)} %constant.212.clone.1), kind=kCustom, calls=%fused_computation.159 | custom fusion | bytes 6656 | tf_op jit(solution)/shard_map/scatter | solution.py:33
  903.4 60.5 %scatter_custom_fusion.5 = f32[1536]{0:T(1024)S(1)} fusion(s32[16384]{0:T(1024)} %get-tuple-element.132, f32[16384]{0:T(1024)S(1)} %reshape.445, f32[]{:T(128)} %constant.229.clone.1), kind=kCustom, calls=%fused_computation.157 | custom fusion | bytes 6656 | tf_op jit(solution)/shard_map/scatter | solution.py:35
  964.0 9.8 gather_fusion.7
  973.8 10.5 gather_fusion.3
  990.3 69.0 %all-reduce.11.cloned.1.call-done = (bf16[2,512,1024]{2,1,0:T(8,128)(2,1)}, bf16[2,1024,512]{2,1,0:T(8,128)(2,1)}, bf16[2,1024,512]{2,1,0:T(8,128)(2,1)}) async-done(((bf16[2,512,1024]{2,1,0:T(8,128)(2,1)}, bf16[2,1024,512]{2,1,0:T(8,128)(2,1)}, bf16[2,1024,512]{2,1,0:T(8,128)(2,1)}), (bf16[2,512,1024]{2,1,0:T(8,128)(2,1)}, bf16[2,1024,512]{2,1,0:T(8,128)(2,1)}, ...) | async-done | bytes 6291472 | tf_op jit(solution)/shard_map/psum | solution.py:101
  1082.1 22.5 copy.32
  1104.7 26.9 convolution_convert_fusion.1
  1131.5 26.4 convolution_convert_fusion.2
  1158.0 317.6 %all-to-all-done.2 = bf16[32,496,1024]{2,1,0:T(8,128)(2,1)} async-done(((bf16[32,496,1024]{2,1,0:T(8,128)(2,1)}), bf16[32,496,1024]{2,1,0:T(8,128)(2,1)}, u32[]{:S(2)}, u32[]{:S(2)}) %all-to-all-start.2) | async-done | bytes 32505888 | tf_op jit(solution)/shard_map/all_to_all | solution.py:109
  1475.5 22.5 copy.37
  1498.0 31.0 fusion.57
  1529.0 41.0 %fusion.10 = (bf16[8,1984,512]{2,1,0:T(8,128)(2,1)}, bf16[8,1984,512]{2,1,0:T(8,128)(2,1)}) fusion(bf16[8,1984,512]{2,1,0:T(8,128)(2,1)} %convolution_convert_fusion.2, bf16[8,1984,512]{2,1,0:T(8,128)(2,1)} %convolution_convert_fusion.1, bf16[8,1984,1024]{2,1,0:T(8,128)(2,1)} %bitcast.103, bf16[8,512,1024]{2,1,0:T(8,128)(2,1)} %param.33), kind=kOutput, calls=%fused_computation.37 | convolution fusion | flops 16764895232 | bytes 105906176 | tf_op jit(solution)/shard_map/esd,efd->esf/dot_general | solution.py:52
  1570.0 11.9 copy.56
  1581.9 32.9 %fusion.62 = f32[8,1984,1024]{2,1,0:T(8,128)} fusion(bf16[8,1984,512]{2,1,0:T(8,128)(2,1)} %get-tuple-element.124, bf16[8,1024,512]{2,1,0:T(8,128)(2,1)} %param.31), kind=kOutput, calls=%fused_computation.168 | convolution fusion | flops 16642998272 | bytes 89653248 | tf_op jit(solution)/shard_map/esf,edf->esd/dot_general | solution.py:58
  1614.8 41.5 %add_convert_fusion = bf16[8,1984,1024]{2,1,0:T(8,128)(2,1)} fusion(f32[8,1984,1024]{2,1,0:T(8,128)} %fusion.62, bf16[8,1984,512]{2,1,0:T(8,128)(2,1)} %get-tuple-element.123, bf16[8,1024,512]{2,1,0:T(8,128)(2,1)} %param.32), kind=kOutput, calls=%fused_computation.17 | convolution fusion | flops 16675504128 | bytes 122159104 | tf_op jit(solution)/shard_map/esf,edf->esd/dot_general | solution.py:59
  1656.2 55.7 %copy.38 = bf16[8,1984,1024]{2,0,1:T(8,128)(2,1)} copy(bf16[8,1984,1024]{2,1,0:T(8,128)(2,1)} %add_convert_fusion) | data formatting | bytes 65011712 | tf_op jit(solution)/shard_map/convert_element_type | solution.py:59
  1711.9 11.5 all-to-all-start.3
  1723.4 28.9 fusion.64
  1752.4 11.8 copy.53
  1764.1 28.6 fusion.66
  1792.7 11.9 copy.52
  1825.9 32.8 %convolution_convert_fusion = bf16[8,1984,1024]{2,1,0:T(8,128)(2,1)} fusion(bf16[8,512,1024]{2,1,0:T(8,128)(2,1)} %param.33, bf16[8,1984,512]{2,1,0:T(8,128)(2,1)} %convolution_convert_fusion.1, bf16[8,1984,512]{2,1,0:T(8,128)(2,1)} %convolution_convert_fusion.2), kind=kOutput, calls=%fused_computation.39 | convolution fusion | flops 16724262912 | bytes 73400320 | tf_op jit(solution)/shard_map/esf,efd->esd/dot_general | solution.py:47
  1858.7 55.6 %copy.33 = bf16[8,1984,1024]{2,0,1:T(8,128)(2,1)} copy(bf16[8,1984,1024]{2,1,0:T(8,128)(2,1)} %convolution_convert_fusion) | data formatting | bytes 65011712 | tf_op jit(solution)/shard_map/convert_element_type | solution.py:47
  1914.3 159.5 %all-to-all-done.3 = bf16[8,1984,1024]{2,0,1:T(8,128)(2,1)} async-done(((bf16[8,1984,1024]{2,0,1:T(8,128)(2,1)}), bf16[8,1984,1024]{2,0,1:T(8,128)(2,1)}, u32[]{:S(2)}, u32[]{:S(2)}) %all-to-all-start.3) | async-done | bytes 32505888 | tf_op jit(solution)/shard_map/all_to_all | solution.py:111
  2073.9 10.6 all-to-all-start.1
  2090.8 69.8 %gather_fusion.8 = bf16[16384,1024]{1,0:T(8,128)(2,1)} fusion(bf16[1536,1024]{1,0:T(8,128)(2,1)S(1)} %bitcast.93, s32[16384]{0:T(1024)S(1)} %get-tuple-element.171), kind=kCustom, calls=%fused_computation.7.clone | custom fusion | bytes 67174400 | tf_op jit(solution)/shard_map/jit(_take)/gather | solution.py:68
  2165.2 69.7 %gather_fusion.4 = bf16[16384,1024]{1,0:T(8,128)(2,1)} fusion(bf16[1536,1024]{1,0:T(8,128)(2,1)S(1)} %bitcast.92, s32[16384]{0:T(1024)S(1)} %get-tuple-element.171), kind=kCustom, calls=%fused_computation.3.clone | custom fusion | bytes 67174400 | tf_op jit(solution)/shard_map/jit(_take)/gather | solution.py:68
  2234.9 22.0 copy.39
  2257.0 177.9 %all-to-all-done.1 = bf16[8,1984,1024]{2,0,1:T(8,128)(2,1)} async-done(((bf16[8,1984,1024]{2,0,1:T(8,128)(2,1)}), bf16[8,1984,1024]{2,0,1:T(8,128)(2,1)}, u32[]{:S(2)}, u32[]{:S(2)}) %all-to-all-start.1) | async-done | bytes 32505888 | tf_op jit(solution)/shard_map/all_to_all | solution.py:105
  2434.9 22.0 copy.34
  2457.0 354.8 %gather_fusion.6 = bf16[16384,1024]{1,0:T(8,128)(2,1)} fusion(bf16[15872,1024]{1,0:T(8,128)(2,1)} %bitcast.94, s32[16384]{0:T(1024)S(1)} %copy-done.10), kind=kCustom, calls=%fused_computation.5.clone | custom fusion | bytes 67174400 | tf_op jit(solution)/shard_map/jit(_take)/gather | solution.py:67
  2811.7 354.9 %gather_fusion.2 = bf16[16384,1024]{1,0:T(8,128)(2,1)} fusion(bf16[15872,1024]{1,0:T(8,128)(2,1)} %bitcast.95, s32[16384]{0:T(1024)S(1)} %copy-done.10), kind=kCustom, calls=%fused_computation.1.clone | custom fusion | bytes 67174400 | tf_op jit(solution)/shard_map/jit(_take)/gather | solution.py:67
  3166.6 28.9 bitcast_reduce_fusion
  3195.5 39.2 %fusion = bf16[2048,1024]{1,0:T(8,128)(2,1)} fusion(bf16[16384,1024]{1,0:T(8,128)(2,1)} %gather_fusion.4, bf16[16384,1024]{1,0:T(8,128)(2,1)} %gather_fusion.2, f32[2048,8]{1,0:T(8,128)S(1)} %copy-done.2, pred[16384]{0:T(1024)(128)(4,1)S(1)} %copy-done.15, pred[16384]{0:T(1024)(128)(4,1)S(1)} %copy-done.14), kind=kLoop, calls=%fused_computation.16 | loop fusion | flops 148897792 | bytes 71401472 | tf_op jit(solution)/shard_map/reduce_sum | solution.py:72
  3234.8 13.5 copy.61
  (118 shorter events, 112.0 us)
Async XLA Ops:
  124.0 185.5 %copy-start.17 = (s32[16384]{0:T(1024)}, s32[16384]{0:T(1024)S(1)}, u32[]{:S(2)}) copy-start(s32[16384]{0:T(1024)S(1)} %add_select_fusion) | copy-start | bytes 196612
  309.5 131.2 %copy-start.11 = (s32[16384]{0:T(1024)}, s32[16384]{0:T(1024)S(1)}, u32[]{:S(2)}) copy-start(s32[16384]{0:T(1024)S(1)} %get-tuple-element.118) | copy-start | bytes 196612
  463.2 360.7 %all-to-all-start = ((bf16[32,496,1024]{2,1,0:T(8,128)(2,1)}), bf16[32,496,1024]{2,1,0:T(8,128)(2,1)}, u32[]{:S(2)}, u32[]{:S(2)}) async-start(bf16[32,496,1024]{2,1,0:T(8,128)(2,1)} %bitcast.96), calls=%async_computation | async-start | bytes 65011712 | tf_op jit(solution)/shard_map/all_to_all | solution.py:103
  473.6 70.9 %copy-start.16 = (f32[2048,8]{0,1:T(8,128)S(1)}, f32[2048,8]{0,1:T(8,128)}, u32[]{:S(2)}) copy-start(f32[2048,8]{0,1:T(8,128)} %param.29) | copy-start | bytes 196612
  544.8 83.3 %copy-start.1 = (f32[2048,8]{1,0:T(8,128)}, f32[2048,8]{1,0:T(8,128)S(1)}, u32[]{:S(2)}) copy-start(f32[2048,8]{1,0:T(8,128)S(1)} %copy.35) | copy-start | bytes 196612
  823.9 651.6 %all-to-all-start.2 = ((bf16[32,496,1024]{2,1,0:T(8,128)(2,1)}), bf16[32,496,1024]{2,1,0:T(8,128)(2,1)}, u32[]{:S(2)}, u32[]{:S(2)}) async-start(bf16[32,496,1024]{2,1,0:T(8,128)(2,1)} %bitcast.97), calls=%async_computation.2 | async-start | bytes 65011712 | tf_op jit(solution)/shard_map/all_to_all | solution.py:109
  834.3 224.9 %all-reduce.11.cloned.1.call-start = ((), (), s32[]{:S(2)}) async-start(), calls=%async_computation.6 | async-start | bytes 12582912 | tf_op jit(solution)/shard_map/psum | solution.py:101
  843.0 961.6 %all-reduce.7.cloned.1.call-start = ((), (), s32[]{:S(2)}) async-start(), calls=%async_computation.4 | async-start | bytes 25165824 | tf_op jit(solution)/shard_map/psum | solution.py:114
  990.3 73.5 %copy-start.6 = (bf16[1536,1024]{1,0:T(8,128)(2,1)S(1)}, bf16[1536,1024]{1,0:T(8,128)(2,1)}, u32[]{:S(2)}) copy-start(bf16[1536,1024]{1,0:T(8,128)(2,1)} %broadcast_select_fusion.1) | copy-start | bytes 9437188
  1059.3 4.5 copy-start.19
  1063.8 14.3 copy-start.21
  1063.8 2.5 copy-start.7
  1063.8 3.7 copy-start.18
  1065.6 8.4 copy-start.23
  1070.1 8.0 copy-start.9
  1070.1 8.0 copy-start.24
  1711.9 361.9 %all-to-all-start.3 = ((bf16[8,1984,1024]{2,0,1:T(8,128)(2,1)}), bf16[8,1984,1024]{2,0,1:T(8,128)(2,1)}, u32[]{:S(2)}, u32[]{:S(2)}) async-start(bf16[8,1984,1024]{2,0,1:T(8,128)(2,1)} %copy.38), calls=%async_computation.3 | async-start | bytes 65011712 | tf_op jit(solution)/shard_map/all_to_all | solution.py:111
  1723.4 1511.3 %all-reduce.9.cloned.1.call-start = ((), (), s32[]{:S(2)}) async-start(), calls=%async_computation.5 | async-start | bytes 100663296 | tf_op jit(solution)/shard_map/psum | solution.py:125
  1804.6 4.4 copy-start.3
  1804.6 8.3 copy-start.4
  1809.0 7.4 copy-start.5
  1914.3 170.2 %copy-start.12 = (s32[16384]{0:T(1024)S(1)}, s32[16384]{0:T(1024)}, u32[]{:S(2)}) copy-start(s32[16384]{0:T(1024)} %copy-done.11) | copy-start | bytes 196612
  1914.3 170.2 %copy-start.13 = (s32[16384]{0:T(1024)S(1)}, s32[16384]{0:T(1024)}, u32[]{:S(2)}) copy-start(s32[16384]{0:T(1024)} %get-tuple-element.132) | copy-start | bytes 196612
  1914.3 170.9 %copy-start.8 = (bf16[2,1024,512]{2,1,0:T(8,128)(2,1)S(1)}, bf16[2,1024,512]{2,1,0:T(8,128)(2,1)}, u32[]{:S(2)}) copy-start(bf16[2,1024,512]{2,1,0:T(8,128)(2,1)} %get-tuple-element.116) | copy-start | bytes 6291460
  2073.9 361.0 %all-to-all-start.1 = ((bf16[8,1984,1024]{2,0,1:T(8,128)(2,1)}), bf16[8,1984,1024]{2,0,1:T(8,128)(2,1)}, u32[]{:S(2)}, u32[]{:S(2)}) async-start(bf16[8,1984,1024]{2,0,1:T(8,128)(2,1)} %copy.33), calls=%async_computation.1 | async-start | bytes 65011712 | tf_op jit(solution)/shard_map/all_to_all | solution.py:105
  2084.5 4.3 copy-start.20
  2084.5 4.3 copy-start.22
  2084.6 4.3 copy-start.25
  2434.9 22.1 copy-start.10
  2811.7 354.9 %copy-start.14 = (pred[16384]{0:T(1024)(128)(4,1)S(1)}, pred[16384]{0:T(1024)(128)(4,1)}, u32[]{:S(2)}) copy-start(pred[16384]{0:T(1024)(128)(4,1)} %get-tuple-element.117) | copy-start | bytes 49156
  2811.7 354.9 %copy-start.15 = (pred[16384]{0:T(1024)(128)(4,1)S(1)}, pred[16384]{0:T(1024)(128)(4,1)}, u32[]{:S(2)}) copy-start(pred[16384]{0:T(1024)(128)(4,1)} %get-tuple-element.131) | copy-start | bytes 49156
  3166.6 28.9 copy-start.2
  3234.8 16.4 copy-start
  3234.8 24.9 slice-start
  3234.8 24.9 slice-start.1
  3251.2 9.9 slice-start.2
  3251.2 11.1 slice-start.3
Sparse Core Ops, SparseCore 0:
  843.1 216.1 all-reduce.10
  1082.2 406.2 all-reduce.6
  1826.0 1094.2 all-reduce.8
where the time goes:
time: 3300 us; the launch traced here: 3280 us
  local copies, waits for them, and re-layouts  1680 us (51%)
  waiting for transfers between devices  920 us (28%)
  matrix products  321 us (10%)
  other arithmetic  297 us (9%)
  starting transfers between devices  42.9 us (1%)
    gather x2, local copies, waits for them, and re-layouts, combine(): jnp.take(cold_vals, cold_rows, axis=0, mode='fill', fill_value=0)  710 us
    all_to_all x1, waiting for transfers between devices, body(): lax.all_to_all(cold_do.reshape(n_exp, cap_cold, d_model), 'expert', 0, 1,...  318 us
    all_to_all x1, waiting for transfers between devices, body(): lax.all_to_all(cold_x.reshape(n_exp, cap_cold, d_model), 'expert', 0, 1,...  196 us
    all_to_all x1, waiting for transfers between devices, body(): back_out = lax.all_to_all(cold_out, 'expert', 1, 0, tiled=True)  178 us
    all_to_all x1, waiting for transfers between devices, body(): back_dx = lax.all_to_all(cold_dx, 'expert', 1, 0, tiled=True)  160 us
    gather x2, local copies, waits for them, and re-layouts, combine(): jnp.take(hot_vals, hot_rows, axis=0, mode='fill', fill_value=0)  140 us
    scatter x2, local copies, waits for them, and re-layouts, gather_rows(): jnp.zeros((n_rows,), jnp.float32).at[slot_rows].set(gate_flat, mode='drop')  121 us
    scatter x2, local copies, waits for them, and re-layouts, gather_rows(): jnp.full((n_rows,), tok_n, jnp.int32).at[slot_rows]  121 us
  transfers between devices with their start and end apart: 7, of which 5 were waited for; matrix products, arithmetic and copies ran while one was open for 55% of the time, Pallas kernels for 0%

commit v1 on v0

v1 whole, which is shorter than its diff:
```python
import functools

import jax
import jax.numpy as jnp
from jax import lax
from jax.experimental import pallas as pl
from jax.experimental.pallas import tpu as pltpu
from jax.sharding import PartitionSpec as P


N_EXP = 32
TOK = 2048
D = 1024
F = 512
LANES = 128
CH = D // LANES
TOP_K = 8
SLOTS = TOK * TOP_K
CAP_COLD = 496
CAP_HOT = 768
CAPS = (CAP_HOT, CAP_COLD, CAP_COLD, CAP_COLD)
LIST = SLOTS + 1024
UNROLL = 8
BF = jnp.bfloat16
F32 = jnp.float32


def gather_kernel(meta, idx, gate, x_ref, dy_ref, *rest):
    x0, x1, d0, d1, xs, ds = rest[-6:]
    g = pl.program_id(0)
    for pos, rows in enumerate(CAPS):
        start = meta[g * 4 + pos]
        cnt = meta[8 + g * 4 + pos]

        def group(i0, carry):
            for u in range(UNROLL):
                i = i0 * UNROLL + u
                t = idx[start + i]
                gt = gate[start + i]
                at = pl.ds(pl.multiple_of(i * CH, CH), CH)
                xs[at, :] = x_ref[t].astype(F32)
                ds[at, :] = dy_ref[t].astype(F32) * gt
            return carry

        lax.fori_loop(0, rows // UNROLL, group, 0)
        live = lax.broadcasted_iota(jnp.int32, (rows, LANES), 0) < cnt
        for k in range(CH):
            xk = xs[pl.ds(k, rows, stride=CH), :].astype(BF)
            dk = jnp.where(live, ds[pl.ds(k, rows, stride=CH), :], 0.0).astype(BF)
            lanes = slice(k * LANES, (k + 1) * LANES)
            if pos == 0:
                x0[0, 0, :, lanes] = xk
                d0[0, 0, :, lanes] = dk
            else:
                x1[0, 0, pos - 1, :, lanes] = xk
                d1[0, 0, pos - 1, :, lanes] = dk


def gather_rows(s, n_src, n_grp, table, x3, dy3, prev):
    meta, idx, gate = table
    smem = pl.BlockSpec(memory_space=pltpu.SMEM)
    whole = pl.BlockSpec((TOK, CH, LANES), lambda g: (0, 0, 0))
    shapes = [jax.ShapeDtypeStruct((n_src, n_grp, CAP_HOT, D), BF),
              jax.ShapeDtypeStruct((n_src, n_grp, 3, CAP_COLD, D), BF)] * 2
    specs = [pl.BlockSpec((1, 1, CAP_HOT, D), lambda g: (s, g, 0, 0)),
             pl.BlockSpec((1, 1, 3, CAP_COLD, D), lambda g: (s, g, 0, 0, 0))] * 2
    args = [meta, idx, gate, x3, dy3]
    in_specs = [smem, smem, smem, whole, whole]
    alias = {}
    if prev is not None:
        alias = {5 + i: i for i in range(4)}
        args += list(prev)
        in_specs += [pl.BlockSpec(memory_space=pl.ANY)] * 4
    return pl.pallas_call(
        gather_kernel, grid=(n_grp,), out_shape=shapes, in_specs=in_specs, out_specs=specs,
        input_output_aliases=alias,
        scratch_shapes=[pltpu.VMEM((CAP_HOT * CH, LANES), F32)] * 2,
        cost_estimate=pl.CostEstimate(flops=n_grp * 10 ** 10, bytes_accessed=n_grp * 10 ** 7, transcendentals=0),
        name="gather_rows",
    )(*args)


def dot(a, b, dims):
    return lax.dot_general(a, b, (dims, ((), ())), preferred_element_type=F32)


NN = ((1,), (0,))
NT = ((1,), (1,))
TN = ((0,), (0,))


def expert_rows(x, do, w1, w3, w2, o, dx, g13, g2):
    pre_a = dot(x, w1, NN).astype(BF)
    pre_b = dot(x, w3, NN).astype(BF)
    dh = dot(do, w2, NT)
    a = pre_a.astype(F32)
    b = pre_b.astype(F32)
    sig = jax.nn.sigmoid(a)
    hid = (a * sig * b).astype(BF)
    db = (dh * a * sig).astype(BF)
    da = (dh * b * sig * (1.0 + a * (1.0 - sig))).astype(BF)
    if o is not None:
        o[...] = dot(hid, w2, NN).astype(BF).reshape(o.shape)
        dx[...] = (dot(da, w1, NT) + dot(db, w3, NT)).astype(BF).reshape(dx.shape)
    if g13 is not None:
        g13[0] += dot(x, da, TN)
        g13[1] += dot(x, db, TN)
        g2[...] += dot(hid, do, TN)


def mine_kernel(first, n_out, q_ref, x, d, fx, fd, w1, w3, w2, *rest):
    outs, g13, g2 = rest[-2 - n_out:-2], rest[-2], rest[-1]
    s = pl.program_id(0)

    @pl.when(s == 0)
    def _():
        g13[...] = jnp.zeros_like(g13)
        g2[...] = jnp.zeros_like(g2)

    rows = x.shape[-2]
    weights = (w1.at[0], w3.at[0], w2.at[0])

    def run(xr, dr, o, dx):
        expert_rows(xr[...].reshape(rows, D), dr[...].reshape(rows, D), *[w[...] for w in weights], o, dx, g13, g2)

    if first == 0:
        @pl.when(s < 2)
        def _():
            run(x, d, outs[0], outs[1])

        @pl.when((s >= 2) & (s < 4))
        def _():
            run(x, d, outs[2], outs[3])
    else:
        @pl.when(s < 2)
        def _():
            run(x, d, None, None)

        @pl.when((s >= 2) & (s < 4))
        def _():
            run(x, d, outs[0], outs[1])

    @pl.when(s >= 4)
    def _():
        run(fx, fd, None, None)


def other_kernel(q_ref, x, d, w1, w3, w2, *rest):
    o, dx = rest[-2:]
    rows = x.shape[-2]
    expert_rows(x[...].reshape(rows, D), d[...].reshape(rows, D), w1[0], w3[0], w2[0], o, dx, None, None)


def w_specs(expert_of):
    return [pl.BlockSpec((1, D, F), lambda *a: (expert_of(*a), 0, 0)),
            pl.BlockSpec((1, D, F), lambda *a: (expert_of(*a), 0, 0)),
            pl.BlockSpec((1, F, D), lambda *a: (expert_of(*a), 0, 0))]


def row_spec(pos, grp, src_of):
    if pos == 0:
        return pl.BlockSpec((1, 1, CAP_HOT, D), lambda *a: (src_of(*a), grp, 0, 0))
    return pl.BlockSpec((1, 1, 1, CAP_COLD, D), lambda *a: (src_of(*a), grp, pos - 1, 0, 0))


def row_shape(pos):
    if pos == 0:
        return jax.ShapeDtypeStruct((2, 2, CAP_HOT, D), BF)
    return jax.ShapeDtypeStruct((2, 2, 3, CAP_COLD, D), BF)


VMEM_LIMIT = 63 * 1024 * 1024


def run_mine(pos, first, q1, x, d, fx, fd, weights, prev):
    own = lambda s, q: jnp.minimum(s, 3)
    far = lambda s, q: jnp.maximum(s - 4, 0)
    near = lambda s, q: jnp.clip(s - 2, 0, 1)
    exp = lambda s, q: q[0] * 4 + pos
    in_specs = [row_spec(pos, 0, own)] * 2 + [row_spec(pos, 0, far)] * 2 + w_specs(exp)
    args = [x, d, fx, fd, *weights]
    out_specs = [row_spec(pos, 0, near)] * 2
    if first == 0:
        out_specs = [row_spec(pos, 0, lambda s, q: jnp.minimum(s, 1))] * 2 + out_specs
    n_out = len(out_specs)
    alias = {}
    if prev is not None:
        alias = {8 + i: i for i in range(n_out)}
        args += list(prev)
        in_specs += [pl.BlockSpec(memory_space=pl.ANY)] * n_out
    rows = CAPS[pos]
    return pl.pallas_call(
        functools.partial(mine_kernel, first, n_out),
        grid_spec=pltpu.PrefetchScalarGridSpec(
            num_scalar_prefetch=1, grid=(8,), in_specs=in_specs,
            out_specs=out_specs + [
                pl.BlockSpec((2, D, F), lambda s, q: (0, 0, 0)),
                pl.BlockSpec((F, D), lambda s, q: (0, 0))]),
        out_shape=[row_shape(pos)] * n_out + [jax.ShapeDtypeStruct((2, D, F), F32),
                                              jax.ShapeDtypeStruct((F, D), F32)],
        input_output_aliases=alias,
        compiler_params=pltpu.CompilerParams(vmem_limit_bytes=VMEM_LIMIT),
        cost_estimate=pl.CostEstimate(flops=2 * rows * 4 * 15 * D * F, bytes_accessed=rows * 50000, transcendentals=0),
        name="mine",
    )(q1, *args)


def run_other(pos0, n_pos, grp, first, q1, x, d, weights, prev):
    exp = lambda p, s, q: (q[0] if grp == 0 else 1 - q[0]) * 4 + pos0 + p

    def spec(s0):
        if pos0 == 0:
            return pl.BlockSpec((1, 1, CAP_HOT, D), lambda p, s, q: (s0 + s, grp, 0, 0))
        return pl.BlockSpec((1, 1, 1, CAP_COLD, D), lambda p, s, q: (s0 + s, grp, pos0 - 1 + p, 0, 0))

    in_specs = [spec(first)] * 2 + w_specs(exp)
    args = [x, d, *weights]
    alias = {}
    if prev is not None:
        alias = {6: 0, 7: 1}
        args += list(prev)
        in_specs += [pl.BlockSpec(memory_space=pl.ANY)] * 2
    rows = CAPS[pos0] * n_pos
    return pl.pallas_call(
        other_kernel,
        grid_spec=pltpu.PrefetchScalarGridSpec(
            num_scalar_prefetch=1, grid=(n_pos, 2), in_specs=in_specs, out_specs=[spec(0)] * 2),
        out_shape=[row_shape(pos0)] * 2,
        input_output_aliases=alias,
        compiler_params=pltpu.CompilerParams(vmem_limit_bytes=VMEM_LIMIT),
        cost_estimate=pl.CostEstimate(flops=2 * rows * 2 * 6 * D * F, bytes_accessed=rows * 25000, transcendentals=0),
        name="other",
    )(q1, *args)


def combine_kernel(gated, has_init, meta, idx, gate, *rest):
    if has_init:
        init, rest = rest[0], rest[1:]
    o0, o1, out, acc, rows_f, sem = rest
    g = pl.program_id(0)
    main = acc.at[pl.ds(0, TOK)]

    @pl.when(g == 0)
    def _():
        if has_init:
            copy = pltpu.make_async_copy(init, main, sem.at[0])
            copy.start()
            copy.wait()
            acc[pl.ds(TOK, UNROLL)] = jnp.zeros((UNROLL, CH, LANES), F32)
        else:
            acc[...] = jnp.zeros_like(acc)

    for pos, rows in enumerate(CAPS):
        start = meta[g * 4 + pos]
        cnt = meta[8 + g * 4 + pos]
        for k in range(CH):
            lanes = slice(k * LANES, (k + 1) * LANES)
            ok = o0[0, 0, :, lanes] if pos == 0 else o1[0, 0, pos - 1, :, lanes]
            rows_f[pl.ds(k, rows, stride=CH), :] = ok.astype(F32)

        def group(i0, carry):
            base = i0 * UNROLL
            toks = [jnp.where(base + u < cnt, idx[start + base + u], TOK + u) for u in range(UNROLL)]
            vals = [rows_f[pl.ds(pl.multiple_of((base + u) * CH, CH), CH), :] for u in range(UNROLL)]
            if gated:
                vals = [v * gate[start + base + u] for u, v in enumerate(vals)]
            sums = [acc[t] + v for t, v in zip(toks, vals)]
            for t, v in zip(toks, sums):
                acc[t] = v
            return carry

        lax.fori_loop(0, (cnt + UNROLL - 1) // UNROLL, group, 0)

    @pl.when(g == 1)
    def _():
        copy = pltpu.make_async_copy(main, out, sem.at[0])
        copy.start()
        copy.wait()


def combine(s, table, rows, gated, init):
    meta, idx, gate = table
    smem = pl.BlockSpec(memory_space=pltpu.SMEM)
    anym = pl.BlockSpec(memory_space=pl.ANY)
    r0 = pl.BlockSpec((1, 1, CAP_HOT, D), lambda g: (s, g, 0, 0))
    r1 = pl.BlockSpec((1, 1, 3, CAP_COLD, D), lambda g: (s, g, 0, 0, 0))
    args = [meta, idx, gate] + ([init] if init is not None else []) + list(rows)
    in_specs = [smem] * 3 + ([anym] if init is not None else []) + [r0, r1]
    return pl.pallas_call(
        functools.partial(combine_kernel, gated, init is not None), grid=(2,),
        out_shape=jax.ShapeDtypeStruct((TOK, CH, LANES), F32),
        in_specs=in_specs, out_specs=anym,
        scratch_shapes=[pltpu.VMEM((TOK + UNROLL, CH, LANES), F32), pltpu.VMEM((CAP_HOT * CH, LANES), F32),
                        pltpu.SemaphoreType.DMA((1,))],
        compiler_params=pltpu.CompilerParams(vmem_limit_bytes=VMEM_LIMIT),
        cost_estimate=pl.CostEstimate(flops=2 * 10 ** 10, bytes_accessed=2 * 10 ** 7, transcendentals=0),
        name="combine",
    )(*args)


def slot_lists(routes, gates):
    flat = routes.reshape(-1)
    key = flat * SLOTS + jnp.arange(SLOTS, dtype=jnp.int32)
    key, gate = lax.sort((key, gates.reshape(-1)), num_keys=1, is_stable=False)
    tok = (key % SLOTS) // TOP_K
    exps = jnp.arange(N_EXP, dtype=jnp.int32)
    counts = jnp.sum((routes[:, :, None] == exps).astype(jnp.int32), axis=(0, 1))
    starts = jnp.sum(jnp.where(exps[None, :] < exps[:, None], counts[None, :], 0), axis=1)
    hot = (exps == 0) | (exps == N_EXP // 2)
    kept = jnp.minimum(counts, jnp.where(hot, CAP_HOT, CAP_COLD))
    pad = jnp.zeros((LIST - SLOTS,), F32)
    return jnp.concatenate([tok.astype(F32), pad, gate, pad, starts.astype(F32), kept.astype(F32)])


def solution(mesh):
    row_spec_p = P(('pod', 'data', 'expert'), None)
    w_spec = P('expert', None, None)
    grad_spec = P(('pod', 'expert'), None, None)

    def core(v):
        return lax.ppermute(v, 'expert', [(i, i ^ 1) for i in range(4)])

    def xhop(v):
        return lax.ppermute(v, 'expert', [(i, i ^ 2) for i in range(4)])

    def yhop(v):
        return lax.ppermute(v, 'data', [(0, 1), (1, 0)])

    def body(tokens, routes, gates, grad_y, w_in1, w_in3, w_out):
        q = lax.axis_index('data')
        r = lax.axis_index('expert')
        q1 = q.reshape(1).astype(jnp.int32)

        x = [tokens.reshape(TOK, CH, LANES)] + [None] * 7
        dy = [grad_y.reshape(TOK, CH, LANES)] + [None] * 7
        x[0], dy[0], routes, gates = lax.optimization_barrier((x[0], dy[0], routes, gates))
        for v in (x, dy):
            v[2] = xhop(v[0])
            v[4] = yhop(v[0])
            v[1] = core(v[0])
        x[6] = xhop(x[4])
        dy[6] = yhop(dy[2])
        for v in (x, dy):
            v[3] = core(v[2])
            v[5] = core(v[4])
            v[7] = core(v[6])

        lists = lax.all_gather(slot_lists(routes, gates), ('data', 'expert'))

        def table(s):
            src = (q ^ (s // 4)) * 4 + (r ^ (s % 4))
            row = lax.dynamic_index_in_dim(lists, src, 0, keepdims=False)
            idx = row[:LIST].astype(jnp.int32)
            bounds = row[2 * LIST:].reshape(2, 4, 2, 4)
            bounds = lax.dynamic_index_in_dim(bounds, r, 1, keepdims=False)
            bounds = jnp.where(q == 0, bounds, bounds[:, ::-1])
            return bounds.reshape(-1).astype(jnp.int32), idx, row[LIST:2 * LIST]

        tables = [table(s) for s in range(8)]

        own = far = None
        for place, src in ((2, 0), (3, 1), (0, 2), (1, 3)):
            own = gather_rows(place, 4, 2, tables[src], x[src], dy[src], own)
        for s in range(4):
            far = gather_rows(s, 4, 1, tables[4 + s], x[4 + s], dy[4 + s], far)
        weights = (w_in1, w_in3, w_out)
        own0, own1 = (own[0], own[2]), (own[1], own[3])
        far0, far1 = (far[0], far[2]), (far[1], far[3])

        *out1, a13, a2 = run_mine(1, 0, q1, *own1, *far1, weights, None)
        *out1, b13, b2 = run_mine(2, 0, q1, *own1, *far1, weights, out1)
        out_a1, out_b1 = out1[:2], out1[2:]
        out_a1 = run_other(3, 1, 0, 0, q1, *own1, weights, out_a1)
        out_a0 = run_other(0, 1, 0, 0, q1, *own0, weights, None)
        out_a0 = run_other(0, 1, 1, 0, q1, *own0, weights, out_a0)
        out_a1 = run_other(1, 3, 1, 0, q1, *own1, weights, out_a1)

        rows_y, rows_d = (out_a0[0], out_a1[0]), (out_a0[1], out_a1[1])
        far_y = core(combine(1, tables[3], rows_y, True, None))
        far_d = core(combine(1, tables[3], rows_d, False, None))
        far_y = xhop(combine(0, tables[2], rows_y, True, far_y))
        far_d = xhop(combine(0, tables[2], rows_d, False, far_d))

        *out_b1, c13, c2 = run_mine(3, 2, q1, *own1, *far1, weights, out_b1)
        *out_b0, d13, d2 = run_mine(0, 2, q1, *own0, *far0, weights, None)
        out_b0 = run_other(0, 1, 1, 2, q1, *own0, weights, out_b0)
        out_b1 = run_other(1, 3, 1, 2, q1, *own1, weights, out_b1)
        rows_y, rows_d = (out_b0[0], out_b1[0]), (out_b0[1], out_b1[1])
        home_y = core(combine(1, tables[1], rows_y, True, None))
        home_d = core(combine(1, tables[1], rows_d, False, None))
        home_y = combine(0, tables[0], rows_y, True, home_y)
        home_d = combine(0, tables[0], rows_d, False, home_d)
        y_out = (home_y + far_y).astype(BF).reshape(TOK, D)
        grad_x = (home_d + far_d).astype(BF).reshape(TOK, D)

        grads = [None] * 4
        for pos, g13, g2 in ((1, a13, a2), (2, b13, b2), (3, c13, c2), (0, d13, d2)):
            grads[pos] = (g13, g2, yhop(g13), yhop(g2))
        grad_1 = jnp.zeros((8, D, F), F32)
        grad_3 = jnp.zeros((8, D, F), F32)
        grad_2 = jnp.zeros((8, F, D), F32)
        for pos in (1, 2, 3, 0):
            g13, g2, h13, h2 = grads[pos]
            for base, v13, v2 in ((q * 4, g13, g2), ((1 - q) * 4, h13, h2)):
                at = (base + pos, 0, 0)
                grad_1 = lax.dynamic_update_slice(grad_1, v13[:1], at)
                grad_3 = lax.dynamic_update_slice(grad_3, v13[1:], at)
                grad_2 = lax.dynamic_update_slice(grad_2, v2[None], at)
        return y_out, grad_x, grad_1, grad_3, grad_2

    return jax.shard_map(body, mesh=mesh,
                         in_specs=(row_spec_p, row_spec_p, row_spec_p, row_spec_p, w_spec, w_spec, w_spec),
                         out_specs=(row_spec_p, row_spec_p, grad_spec, grad_spec, grad_spec),
                         check_vma=False)
```

time: 3300 us -> 1390 us (0.42)
  local copies, waits for them, and re-layouts: 1680 us -> 99.5 us
  Pallas kernels: 0 us -> 684 us
  waiting for transfers between devices: 920 us -> 537 us
  matrix products: 321 us -> 0 us
  other arithmetic: 297 us -> 19.9 us
    gather x11 -> x0, local copies, waits for them, and re-layouts: 1100 us -> none  [the longest x2 710 us: combine(): jnp.take(cold_vals, cold_rows, axis=0, mode='fill', fill_value=0)]
    all_to_all x4 -> x0, waiting for transfers between devices: 851 us -> none  [the longest x1 318 us: body(): lax.all_to_all(cold_do.reshape(n_exp, cap_cold, d_model), 'expert', 0, 1,...]
    pallas_call x0 -> x26, Pallas kernels: none -> 684 us  [the longest x8 207 us: combine(): pl.pallas_call(functools.partial(combine_kernel, gated, init is not None)...]
    ppermute x0 -> x28, waiting for transfers between devices: none -> 489 us  [the longest x5 267 us: xhop(): return lax.ppermute(v, 'expert', [(i, i ^ 2) for i in range(4)])]
    dot_general x18 -> x0, matrix products: 321 us -> none  [the longest x2 43.6 us: expert_bwd(): jnp.einsum('esd,efd->esf', do_rows, w_c, preferred_element_type=jnp.float32)]
    scatter x5 -> x0, local copies, waits for them, and re-layouts: 302 us -> none  [the longest x2 121 us: gather_rows(): jnp.zeros((n_rows,), jnp.float32).at[slot_rows].set(gate_flat, mode='drop')]
    scatter-add x6 -> x0, other arithmetic: 135 us -> none  [the longest x1 113 us: route_rows(): jax.ops.segment_sum(jnp.ones((n_slots,), jnp.int32), flat_exp, num_segmen...]
    convert_element_type x2 -> x8, local copies, waits for them, and re-layouts: 111 us -> 5.11 us  [table(): return (bounds.reshape(-1).astype(jnp.int32), idx, row[LIST:2 * LIST])]
  transfers between devices with their start and end apart: 7 -> 29, of which waited for: 5 -> 9; matrix products, arithmetic and copies ran while one was open for 55% -> 7% of each run, Pallas kernels for 0% -> 37%
where the time goes in v1:
time: 1390 us; the launch traced here: 1380 us
  Pallas kernels  684 us (49%)
  waiting for transfers between devices  537 us (39%)
  local copies, waits for them, and re-layouts  99.5 us (7%)
  starting transfers between devices  20.6 us (1%)
  other arithmetic  19.9 us (1%)
  between operations  14.7 us (1%)
    ppermute x5, waiting for transfers between devices, xhop(): return lax.ppermute(v, 'expert', [(i, i ^ 2) for i in range(4)])  267 us
    ppermute x11, waiting for transfers between devices, yhop(): return lax.ppermute(v, 'data', [(0, 1), (1, 0)])  222 us
    pallas_call x8, Pallas kernels, combine(): pl.pallas_call(functools.partial(combine_kernel, gated, init is not None)...  207 us
    pallas_call x4, Pallas kernels, run_mine(): pl.pallas_call(functools.partial(mine_kernel, first, n_out), grid_spec=pl...  189 us
    pallas_call x8, Pallas kernels, gather_rows(): pl.pallas_call(gather_kernel, grid=(n_grp,), out_shape=shapes, in_specs=i...  180 us
    pallas_call x6, Pallas kernels, run_other(): pl.pallas_call(other_kernel, grid_spec=pltpu.PrefetchScalarGridSpec(num_s...  107 us
    unnamed x2, waiting for transfers between devices  48.7 us
  transfers between devices with their start and end apart: 29, of which 9 were waited for; matrix products, arithmetic and copies ran while one was open for 7% of the time, Pallas kernels for 37%

profile of v1, /device:TPU:5, one launch (start us, length us, event | category | flops | bytes accessed | tf_op | source)
XLA Modules:
  0.0 1375.9 jit_solution(1408488620877177115)
XLA Ops:
  7.2 5.5 copy.58
  18.0 6.5 sort.15
  29.9 48.6 %all-reduce.3.cloned.1.call-done = f32[279040]{0:T(1024)} async-done(((f32[279040]{0:T(1024)}), f32[279040]{0:T(1024)}) %all-reduce.3.cloned.1.call-update) | async-done | bytes 1116176
  87.6 28.1 %gather_rows.8 = (bf16[4,2,768,1024]{3,2,1,0:T(8,128)(2,1)}, bf16[4,2,3,496,1024]{4,3,2,1,0:T(8,128)(2,1)}, bf16[4,2,768,1024]{3,2,1,0:T(8,128)(2,1)}, bf16[4,2,3,496,1024]{4,3,2,1,0:T(8,128)(2,1)}) custom-call(s32[16]{0:T(128)} %convert_element_type.103.meta, s32[17408]{0:T(1024)} %bitcast.99, f32[17408]{0:T(1024)} %bitcast.102, ...), custom_call_target="tpu_custom_call" | custom-call | flops 20000000000 | bytes 20000000 | tf_op jit(solution)/shard_map/gather_rows/pallas_call | solution.py:74
  115.7 15.7 %collective-permute-done.x_ref = bf16[2048,8,128]{2,1,0:T(8,128)(2,1)} collective-permute-done((bf16[2048,8,128]{2,1,0:T(8,128)(2,1)}, bf16[2048,8,128]{2,1,0:T(8,128)(2,1)}, u32[]{:S(2)}, u32[]{:S(2)}) %collective-permute-start) | collective-permute-done | bytes 4194336 | tf_op jit(solution)/shard_map/ppermute | solution.py:324
  131.7 89.6 %collective-permute-done.2.dy_ref = bf16[2048,8,128]{2,1,0:T(8,128)(2,1)} collective-permute-done((bf16[2048,8,128]{2,1,0:T(8,128)(2,1)}, bf16[2048,8,128]{2,1,0:T(8,128)(2,1)}, u32[]{:S(2)}, u32[]{:S(2)}) %collective-permute-start.2) | collective-permute-done | bytes 4194336 | tf_op jit(solution)/shard_map/ppermute | solution.py:324
  225.3 28.2 %gather_rows.9 = (bf16[4,2,768,1024]{3,2,1,0:T(8,128)(2,1)}, bf16[4,2,3,496,1024]{4,3,2,1,0:T(8,128)(2,1)}, bf16[4,2,768,1024]{3,2,1,0:T(8,128)(2,1)}, bf16[4,2,3,496,1024]{4,3,2,1,0:T(8,128)(2,1)}) custom-call(s32[16]{0:T(128)} %convert_element_type.107.meta, ...), custom_call_target="tpu_custom_call", output_to_operand_aliasing={{0}: (5, {}), {1}: (6, {}), {2}: (7, {}), {3}: (8, {})} | custom-call | flops 20000000000 | bytes 20000000 | tf_op jit(solution)/shard_map/gather_rows/pallas_call | solution.py:74
  253.6 27.7 %gather_rows.10 = (bf16[4,2,768,1024]{3,2,1,0:T(8,128)(2,1)}, bf16[4,2,3,496,1024]{4,3,2,1,0:T(8,128)(2,1)}, bf16[4,2,768,1024]{3,2,1,0:T(8,128)(2,1)}, bf16[4,2,3,496,1024]{4,3,2,1,0:T(8,128)(2,1)}) custom-call(s32[16]{0:T(128)} %convert_element_type.115.meta, ...), custom_call_target="tpu_custom_call", output_to_operand_aliasing={{0}: (5, {}), {1}: (6, {}), {2}: (7, {}), {3}: (8, {})} | custom-call | flops 20000000000 | bytes 20000000 | tf_op jit(solution)/shard_map/gather_rows/pallas_call | solution.py:74
  282.4 17.3 %gather_rows.12 = (bf16[4,1,768,1024]{3,2,1,0:T(8,128)(2,1)}, bf16[4,1,3,496,1024]{4,3,2,1,0:T(8,128)(2,1)}, bf16[4,1,768,1024]{3,2,1,0:T(8,128)(2,1)}, bf16[4,1,3,496,1024]{4,3,2,1,0:T(8,128)(2,1)}) custom-call(s32[16]{0:T(128)} %convert_element_type.131.meta, s32[17408]{0:T(1024)} %bitcast.106, f32[17408]{0:T(1024)} %bitcast.105, ...), custom_call_target="tpu_custom_call" | custom-call | flops 10000000000 | bytes 10000000 | tf_op jit(solution)/shard_map/gather_rows/pallas_call | solution.py:74
  299.8 16.3 %collective-permute-done.7.x_ref = bf16[2048,8,128]{2,1,0:T(8,128)(2,1)} collective-permute-done((bf16[2048,8,128]{2,1,0:T(8,128)(2,1)}, bf16[2048,8,128]{2,1,0:T(8,128)(2,1)}, u32[]{:S(2)}, u32[]{:S(2)}) %collective-permute-start.7) | collective-permute-done | bytes 4194336 | tf_op jit(solution)/shard_map/ppermute | solution.py:324
  317.6 28.2 %gather_rows.11 = (bf16[4,2,768,1024]{3,2,1,0:T(8,128)(2,1)}, bf16[4,2,3,496,1024]{4,3,2,1,0:T(8,128)(2,1)}, bf16[4,2,768,1024]{3,2,1,0:T(8,128)(2,1)}, bf16[4,2,3,496,1024]{4,3,2,1,0:T(8,128)(2,1)}) custom-call(s32[16]{0:T(128)} %convert_element_type.111.meta, ...), custom_call_target="tpu_custom_call", output_to_operand_aliasing={{0}: (5, {}), {1}: (6, {}), {2}: (7, {}), {3}: (8, {})} | custom-call | flops 20000000000 | bytes 20000000 | tf_op jit(solution)/shard_map/gather_rows/pallas_call | solution.py:74
  345.8 15.2 %other.8 = (bf16[2,2,768,1024]{3,2,1,0:T(8,128)(2,1)}, bf16[2,2,768,1024]{3,2,1,0:T(8,128)(2,1)}) custom-call(s32[1]{0:T(128)} %bitcast.6.q_ref, bf16[4,2,768,1024]{3,2,1,0:T(8,128)(2,1)} %get-tuple-element.93.x, bf16[4,2,768,1024]{3,2,1,0:T(8,128)(2,1)} %get-tuple-element.94.d, bf16[8,1024,512]{2,1,0:T(8,128)(2,1)} %w1.19, bf16[8,1024,512]{2,1,0:T(8,128)(2,1)} %w3.19, ...), custom_call_target="tpu_custom_call" | custom-call | flops 9663676416 | bytes 19200000 | tf_op jit(solution)/shard_map/other/pallas_call | solution.py:224
  361.0 14.9 %other.9 = (bf16[2,2,768,1024]{3,2,1,0:T(8,128)(2,1)}, bf16[2,2,768,1024]{3,2,1,0:T(8,128)(2,1)}) custom-call(s32[1]{0:T(128)} %bitcast.6.q_ref, bf16[4,2,768,1024]{3,2,1,0:T(8,128)(2,1)} %get-tuple-element.93.x, bf16[4,2,768,1024]{3,2,1,0:T(8,128)(2,1)} %get-tuple-element.94.d, ...), custom_call_target="tpu_custom_call", output_to_operand_aliasing={{0}: (6, {}), {1}: (7, {})} | custom-call | flops 9663676416 | bytes 19200000 | tf_op jit(solution)/shard_map/other/pallas_call | solution.py:224
  375.9 17.1 %gather_rows.13 = (bf16[4,1,768,1024]{3,2,1,0:T(8,128)(2,1)}, bf16[4,1,3,496,1024]{4,3,2,1,0:T(8,128)(2,1)}, bf16[4,1,768,1024]{3,2,1,0:T(8,128)(2,1)}, bf16[4,1,3,496,1024]{4,3,2,1,0:T(8,128)(2,1)}) custom-call(s32[16]{0:T(128)} %convert_element_type.127.meta, ...), custom_call_target="tpu_custom_call", output_to_operand_aliasing={{0}: (5, {}), {1}: (6, {}), {2}: (7, {}), {3}: (8, {})} | custom-call | flops 10000000000 | bytes 10000000 | tf_op jit(solution)/shard_map/gather_rows/pallas_call | solution.py:74
  393.0 16.8 %gather_rows.14 = (bf16[4,1,768,1024]{3,2,1,0:T(8,128)(2,1)}, bf16[4,1,3,496,1024]{4,3,2,1,0:T(8,128)(2,1)}, bf16[4,1,768,1024]{3,2,1,0:T(8,128)(2,1)}, bf16[4,1,3,496,1024]{4,3,2,1,0:T(8,128)(2,1)}) custom-call(s32[16]{0:T(128)} %convert_element_type.123.meta, ...), custom_call_target="tpu_custom_call", output_to_operand_aliasing={{0}: (5, {}), {1}: (6, {}), {2}: (7, {}), {3}: (8, {})} | custom-call | flops 10000000000 | bytes 10000000 | tf_op jit(solution)/shard_map/gather_rows/pallas_call | solution.py:74
  409.8 17.0 %gather_rows.15 = (bf16[4,1,768,1024]{3,2,1,0:T(8,128)(2,1)}, bf16[4,1,3,496,1024]{4,3,2,1,0:T(8,128)(2,1)}, bf16[4,1,768,1024]{3,2,1,0:T(8,128)(2,1)}, bf16[4,1,3,496,1024]{4,3,2,1,0:T(8,128)(2,1)}) custom-call(s32[16]{0:T(128)} %convert_element_type.119.meta, ...), custom_call_target="tpu_custom_call", output_to_operand_aliasing={{0}: (5, {}), {1}: (6, {}), {2}: (7, {}), {3}: (8, {})} | custom-call | flops 10000000000 | bytes 10000000 | tf_op jit(solution)/shard_map/gather_rows/pallas_call | solution.py:74
  426.8 45.1 %mine.5 = (bf16[2,2,3,496,1024]{4,3,2,1,0:T(8,128)(2,1)}, bf16[2,2,3,496,1024]{4,3,2,1,0:T(8,128)(2,1)}, bf16[2,2,3,496,1024]{4,3,2,1,0:T(8,128)(2,1)}, bf16[2,2...) custom-call(s32[1]{0:T(128)} %bitcast.6.q_ref, ...), custom_call_target="tpu_custom_call" | custom-call | flops 31205621760 | bytes 24800000 | tf_op jit(solution)/shard_map/mine/pallas_call | solution.py:192
  471.9 44.8 %mine.6 = (bf16[2,2,3,496,1024]{4,3,2,1,0:T(8,128)(2,1)}, bf16[2,2,3,496,1024]{4,3,2,1,0:T(8,128)(2,1)}, bf16[2,2,3,496,1024]{4,3,2,1,0:T(8,128)(2,1)}, bf16[2,2...) custom-call(s32[1]{0:T(128)} %bitcast.6.q_ref, ...), custom_call_target="tpu_custom_call", output_to_operand_aliasing={{0}: (8, {}), {1}: (9, {}), {2}: (10, {}), {3}: (11, {})} | custom-call | flops 31205621760 | bytes 24800000 | tf_op jit(solution)/shard_map/mine/pallas_call | solution.py:192
  516.7 10.9 other.10
  527.7 25.4 %other.11 = (bf16[2,2,3,496,1024]{4,3,2,1,0:T(8,128)(2,1)}, bf16[2,2,3,496,1024]{4,3,2,1,0:T(8,128)(2,1)}) custom-call(s32[1]{0:T(128)} %bitcast.6.q_ref, bf16[4,2,3,496,1024]{4,3,2,1,0:T(8,128)(2,1)} %get-tuple-element.112.x, bf16[4,2,3,496,1024]{4,3,2,1,0:T(8,128)(2,1)} %get-tuple-element.113.d, ...), custom_call_target="tpu_custom_call", output_to_operand_aliasing={{0}: (6, {}), {1}: (7, {})} | custom-call | flops 18723373056 | bytes 37200000 | tf_op jit(solution)/shard_map/other/pallas_call | solution.py:224
  553.1 26.0 %combine.10 = f32[2048,8,128]{2,1,0:T(8,128)} custom-call(s32[16]{0:T(128)} %convert_element_type.111.meta, s32[17408]{0:T(1024)} %bitcast.88, f32[17408]{0:T(1024)} %bitcast.91, bf16[2,2,768,1024]{3,2,1,0:T(8,128)(2,1)} %get-tuple-element.127.rest_0_.rest_1_, bf16[2,2,3,496,1024]{4,3,2,1,0:T(8,128)(2,1)} %get-tuple-element.132.rest_1_.rest_2_), custom_call_target="tpu_custom_call" | custom-call | flops 20000000000 | bytes 20000000 | tf_op jit(solution)/shard_map/combine/pallas_call | solution.py:289
  579.5 22.5 %combine.14 = f32[2048,8,128]{2,1,0:T(8,128)} custom-call(s32[16]{0:T(128)} %convert_element_type.111.meta, s32[17408]{0:T(1024)} %bitcast.89, f32[17408]{0:T(1024)} %bitcast.92, bf16[2,2,768,1024]{3,2,1,0:T(8,128)(2,1)} %get-tuple-element.135.rest_0_.rest_1_, bf16[2,2,3,496,1024]{4,3,2,1,0:T(8,128)(2,1)} %get-tuple-element.136.rest_1_.rest_2_), custom_call_target="tpu_custom_call" | custom-call | flops 20000000000 | bytes 20000000 | tf_op jit(solution)/shard_map/combine/pallas_call | solution.py:289
  604.9 58.8 %mine.4 = (bf16[2,2,768,1024]{3,2,1,0:T(8,128)(2,1)}, bf16[2,2,768,1024]{3,2,1,0:T(8,128)(2,1)}, f32[2,1024,512]{2,1,0:T(8,128)}, f32[512,1024]{1,0:T(8,128)}) custom-call(s32[1]{0:T(128)} %bitcast.6.q_ref, bf16[4,2,768,1024]{3,2,1,0:T(8,128)(2,1)} %get-tuple-element.93.x, bf16[4,2,768,1024]{3,2,1,0:T(8,128)(2,1)} %get-tuple-element.94.d, ...), custom_call_target="tpu_custom_call" | custom-call | flops 48318382080 | bytes 38400000 | tf_op jit(solution)/shard_map/mine/pallas_call | solution.py:192
  663.7 40.7 %mine.7 = (bf16[2,2,3,496,1024]{4,3,2,1,0:T(8,128)(2,1)}, bf16[2,2,3,496,1024]{4,3,2,1,0:T(8,128)(2,1)}, f32[2,1024,512]{2,1,0:T(8,128)}, f32[512,1024]{1,0:T(8,128)}) custom-call(s32[1]{0:T(128)} %bitcast.6.q_ref, bf16[4,2,3,496,1024]{4,3,2,1,0:T(8,128)(2,1)} %get-tuple-element.112.x, ...), custom_call_target="tpu_custom_call", output_to_operand_aliasing={{0}: (8, {}), {1}: (9, {})} | custom-call | flops 31205621760 | bytes 24800000 | tf_op jit(solution)/shard_map/mine/pallas_call | solution.py:192
  704.5 15.2 %other.6 = (bf16[2,2,768,1024]{3,2,1,0:T(8,128)(2,1)}, bf16[2,2,768,1024]{3,2,1,0:T(8,128)(2,1)}) custom-call(s32[1]{0:T(128)} %bitcast.6.q_ref, bf16[4,2,768,1024]{3,2,1,0:T(8,128)(2,1)} %get-tuple-element.93.x, bf16[4,2,768,1024]{3,2,1,0:T(8,128)(2,1)} %get-tuple-element.94.d, ...), custom_call_target="tpu_custom_call", output_to_operand_aliasing={{0}: (6, {}), {1}: (7, {})} | custom-call | flops 9663676416 | bytes 19200000 | tf_op jit(solution)/shard_map/other/pallas_call | solution.py:224
  722.1 8.8 broadcast.22.clone.1
  734.8 25.4 %other.7 = (bf16[2,2,3,496,1024]{4,3,2,1,0:T(8,128)(2,1)}, bf16[2,2,3,496,1024]{4,3,2,1,0:T(8,128)(2,1)}) custom-call(s32[1]{0:T(128)} %bitcast.6.q_ref, bf16[4,2,3,496,1024]{4,3,2,1,0:T(8,128)(2,1)} %get-tuple-element.112.x, bf16[4,2,3,496,1024]{4,3,2,1,0:T(8,128)(2,1)} %get-tuple-element.113.d, ...), custom_call_target="tpu_custom_call", output_to_operand_aliasing={{0}: (6, {}), {1}: (7, {})} | custom-call | flops 18723373056 | bytes 37200000 | tf_op jit(solution)/shard_map/other/pallas_call | solution.py:224
  760.3 8.3 broadcast_in_dim.60
  770.1 26.5 %combine.8 = f32[2048,8,128]{2,1,0:T(8,128)} custom-call(s32[16]{0:T(128)} %convert_element_type.107.meta, s32[17408]{0:T(1024)} %bitcast.82, f32[17408]{0:T(1024)} %bitcast.85, bf16[2,2,768,1024]{3,2,1,0:T(8,128)(2,1)} %get-tuple-element.111.rest_0_.rest_1_, bf16[2,2,3,496,1024]{4,3,2,1,0:T(8,128)(2,1)} %get-tuple-element.124.rest_1_.rest_2_), custom_call_target="tpu_custom_call" | custom-call | flops 20000000000 | bytes 20000000 | tf_op jit(solution)/shard_map/combine/pallas_call | solution.py:289
  798.0 30.9 %collective-permute-done.26 = f32[512,1024]{1,0:T(8,128)} collective-permute-done((f32[512,1024]{1,0:T(8,128)}, f32[512,1024]{1,0:T(8,128)}, u32[]{:S(2)}, u32[]{:S(2)}) %collective-permute-start.26) | collective-permute-done | bytes 2097184 | tf_op jit(solution)/shard_map/ppermute | solution.py:327
  830.3 22.5 %combine.12 = f32[2048,8,128]{2,1,0:T(8,128)} custom-call(s32[16]{0:T(128)} %convert_element_type.107.meta, s32[17408]{0:T(1024)} %bitcast.83, f32[17408]{0:T(1024)} %bitcast.86, bf16[2,2,768,1024]{3,2,1,0:T(8,128)(2,1)} %get-tuple-element.133.rest_0_.rest_1_, bf16[2,2,3,496,1024]{4,3,2,1,0:T(8,128)(2,1)} %get-tuple-element.134.rest_1_.rest_2_), custom_call_target="tpu_custom_call" | custom-call | flops 20000000000 | bytes 20000000 | tf_op jit(solution)/shard_map/combine/pallas_call | solution.py:289
  852.9 3.2 bitcast_dynamic-update-slice_fusion.6
  856.0 107.7 %collective-permute-done.27 = f32[512,1024]{1,0:T(8,128)} collective-permute-done((f32[512,1024]{1,0:T(8,128)}, f32[512,1024]{1,0:T(8,128)}, u32[]{:S(2)}, u32[]{:S(2)}) %collective-permute-start.27) | collective-permute-done | bytes 2097184 | tf_op jit(solution)/shard_map/ppermute | solution.py:327
  973.0 29.0 %combine.11 = f32[2048,8,128]{2,1,0:T(8,128)} custom-call(s32[16]{0:T(128)} %convert_element_type.115.meta, s32[17408]{0:T(1024)} %bitcast.76, f32[17408]{0:T(1024)} %bitcast.79, f32[2048,8,128]{2,1,0:T(8,128)} %collective-permute-done.15.rest_0_, bf16[2,2,768,1024]{3,2,1,0:T(8,128)(2,1)} %get-tuple-element.127.rest_0_.rest_1_, ...), custom_call_target="tpu_custom_call" | custom-call | flops 20000000000 | bytes 20000000 | tf_op jit(solution)/shard_map/combine/pallas_call | solution.py:289
  1002.2 25.7 %combine.15 = f32[2048,8,128]{2,1,0:T(8,128)} custom-call(s32[16]{0:T(128)} %convert_element_type.115.meta, s32[17408]{0:T(1024)} %bitcast.77, f32[17408]{0:T(1024)} %bitcast.80, f32[2048,8,128]{2,1,0:T(8,128)} %collective-permute-done.18.rest_0_, bf16[2,2,768,1024]{3,2,1,0:T(8,128)(2,1)} %get-tuple-element.135.rest_0_.rest_1_, ...), custom_call_target="tpu_custom_call" | custom-call | flops 20000000000 | bytes 20000000 | tf_op jit(solution)/shard_map/combine/pallas_call | solution.py:289
  1027.8 29.6 %collective-permute-done.22 = f32[2,1024,512]{2,1,0:T(8,128)} collective-permute-done((f32[2,1024,512]{2,1,0:T(8,128)}, f32[2,1024,512]{2,1,0:T(8,128)}, u32[]{:S(2)}, u32[]{:S(2)}) %collective-permute-start.22) | collective-permute-done | bytes 4194336 | tf_op jit(solution)/shard_map/ppermute | solution.py:327
  1068.1 3.7 bitcast_dynamic-update-slice_fusion
  1071.8 4.7 slice_dynamic-update-slice_fusion.3
  1079.0 4.9 slice_dynamic-update-slice_fusion.2
  1086.5 4.9 slice_dynamic-update-slice_fusion.1
  1093.8 53.5 %collective-permute-done.23 = f32[2,1024,512]{2,1,0:T(8,128)} collective-permute-done((f32[2,1024,512]{2,1,0:T(8,128)}, f32[2,1024,512]{2,1,0:T(8,128)}, u32[]{:S(2)}, u32[]{:S(2)}) %collective-permute-start.23) | collective-permute-done | bytes 4194336 | tf_op jit(solution)/shard_map/ppermute | solution.py:327
  1147.3 4.7 slice_dynamic-update-slice_fusion
  1152.0 29.1 %combine.9 = f32[2048,8,128]{2,1,0:T(8,128)} custom-call(s32[16]{0:T(128)} %convert_element_type.103.meta, s32[17408]{0:T(1024)} %bitcast.100, f32[17408]{0:T(1024)} %bitcast.103, f32[2048,8,128]{2,1,0:T(8,128)} %collective-permute-done.14.rest_0_, bf16[2,2,768,1024]{3,2,1,0:T(8,128)(2,1)} %get-tuple-element.111.rest_0_.rest_1_, ...), custom_call_target="tpu_custom_call" | custom-call | flops 20000000000 | bytes 20000000 | tf_op jit(solution)/shard_map/combine/pallas_call | solution.py:289
  1181.1 25.5 %combine.13 = f32[2048,8,128]{2,1,0:T(8,128)} custom-call(s32[16]{0:T(128)} %convert_element_type.103.meta, s32[17408]{0:T(1024)} %bitcast.101, f32[17408]{0:T(1024)} %bitcast.104, f32[2048,8,128]{2,1,0:T(8,128)} %collective-permute-done.17.rest_0_, bf16[2,2,768,1024]{3,2,1,0:T(8,128)(2,1)} %get-tuple-element.133.rest_0_.rest_1_, ...), custom_call_target="tpu_custom_call" | custom-call | flops 20000000000 | bytes 20000000 | tf_op jit(solution)/shard_map/combine/pallas_call | solution.py:289
  1206.6 6.3 add_convert_fusion.1
  1213.0 3.3 copy.65
  1216.2 145.5 %collective-permute-done.19 = f32[2048,8,128]{2,1,0:T(8,128)} collective-permute-done((f32[2048,8,128]{2,1,0:T(8,128)}, f32[2048,8,128]{2,1,0:T(8,128)}, u32[]{:S(2)}, u32[]{:S(2)}) %collective-permute-start.19) | collective-permute-done | bytes 8388640 | tf_op jit(solution)/shard_map/ppermute | solution.py:324
  1361.7 4.1 add_convert_fusion
  (142 shorter events, 71.4 us)
Async XLA Ops:
  7.2 71.4 %all-reduce.3.cloned.1.call-start = ((), (), s32[]{:S(2)}) async-start(), calls=%async_computation | async-start | bytes 2236416
  7.2 5.5 copy-start.3
  7.2 8.6 copy-start.10
  7.2 9.9 copy-start.11
  26.1 1.0 copy-start.2
  27.1 104.3 %collective-permute-start = (bf16[2048,8,128]{2,1,0:T(8,128)(2,1)}, bf16[2048,8,128]{2,1,0:T(8,128)(2,1)}, u32[]{:S(2)}, u32[]{:S(2)}) collective-permute-start(bf16[2048,8,128]{2,1,0:T(8,128)(2,1)} %bitcast.69), channel_id=1, source_target_pairs={{0,2},{1,3},{2,0},{3,1},{4,6},{5,7},{6,4},{7,5}} | collective-permute-start | bytes 12582920 | tf_op jit(solution)/shard_map/ppermute | solution.py:324
  28.2 196.0 %collective-permute-start.4 = (bf16[2048,8,128]{2,1,0:T(8,128)(2,1)}, bf16[2048,8,128]{2,1,0:T(8,128)(2,1)}, u32[]{:S(2)}, u32[]{:S(2)}) collective-permute-start(bf16[2048,8,128]{2,1,0:T(8,128)(2,1)} %bitcast.70), channel_id=1, source_target_pairs={{0,1},{1,0},{2,3},{3,2},{4,5},{5,4},{6,7},{7,6}} | collective-permute-start | bytes 12582920 | tf_op jit(solution)/shard_map/ppermute | solution.py:321
  29.3 192.0 %collective-permute-start.2 = (bf16[2048,8,128]{2,1,0:T(8,128)(2,1)}, bf16[2048,8,128]{2,1,0:T(8,128)(2,1)}, u32[]{:S(2)}, u32[]{:S(2)}) collective-permute-start(bf16[2048,8,128]{2,1,0:T(8,128)(2,1)} %bitcast.65), channel_id=1, source_target_pairs={{0,2},{1,3},{2,0},{3,1},{4,6},{5,7},{6,4},{7,5}} | collective-permute-start | bytes 12582920 | tf_op jit(solution)/shard_map/ppermute | solution.py:324
  29.6 194.6 %collective-permute-start.5 = (bf16[2048,8,128]{2,1,0:T(8,128)(2,1)}, bf16[2048,8,128]{2,1,0:T(8,128)(2,1)}, u32[]{:S(2)}, u32[]{:S(2)}) collective-permute-start(bf16[2048,8,128]{2,1,0:T(8,128)(2,1)} %bitcast.66), channel_id=1, source_target_pairs={{0,1},{1,0},{2,3},{3,2},{4,5},{5,4},{6,7},{7,6}} | collective-permute-start | bytes 12582920 | tf_op jit(solution)/shard_map/ppermute | solution.py:321
  29.9 194.4 %collective-permute-start.6 = (bf16[2048,8,128]{2,1,0:T(8,128)(2,1)}, bf16[2048,8,128]{2,1,0:T(8,128)(2,1)}, u32[]{:S(2)}, u32[]{:S(2)}) collective-permute-start(bf16[2048,8,128]{2,1,0:T(8,128)(2,1)} %bitcast.71), channel_id=1, source_target_pairs={{0,4},{4,0},{1,5},{5,1},{2,6},{6,2},{3,7},{7,3}} | collective-permute-start | bytes 12582920 | tf_op jit(solution)/shard_map/ppermute | solution.py:327
  131.4 149.9 %collective-permute-start.12 = (bf16[2048,8,128]{2,1,0:T(8,128)(2,1)}, bf16[2048,8,128]{2,1,0:T(8,128)(2,1)}, u32[]{:S(2)}, u32[]{:S(2)}) collective-permute-start(bf16[2048,8,128]{2,1,0:T(8,128)(2,1)} %bitcast.68), channel_id=1, source_target_pairs={{0,4},{4,0},{1,5},{5,1},{2,6},{6,2},{3,7},{7,3}} | collective-permute-start | bytes 12582920 | tf_op jit(solution)/shard_map/ppermute | solution.py:327
  221.3 61.1 %collective-permute-start.1 = (bf16[2048,8,128]{2,1,0:T(8,128)(2,1)}, bf16[2048,8,128]{2,1,0:T(8,128)(2,1)}, u32[]{:S(2)}, u32[]{:S(2)}) collective-permute-start(bf16[2048,8,128]{2,1,0:T(8,128)(2,1)} %collective-permute-done.x_ref), channel_id=1, source_target_pairs={{0,1},{1,0},{2,3},{3,2},{4,5},{5,4},{6,7},{7,6}} | collective-permute-start | bytes 12582920 | tf_op jit(solution)/shard_map/ppermute | solution.py:321
  224.2 93.4 %collective-permute-start.3 = (bf16[2048,8,128]{2,1,0:T(8,128)(2,1)}, bf16[2048,8,128]{2,1,0:T(8,128)(2,1)}, u32[]{:S(2)}, u32[]{:S(2)}) collective-permute-start(bf16[2048,8,128]{2,1,0:T(8,128)(2,1)} %collective-permute-done.2.dy_ref), channel_id=1, source_target_pairs={{0,1},{1,0},{2,3},{3,2},{4,5},{5,4},{6,7},{7,6}} | collective-permute-start | bytes 12582920 | tf_op jit(solution)/shard_map/ppermute | solution.py:321
  224.2 93.4 %collective-permute-start.9 = (bf16[2048,8,128]{2,1,0:T(8,128)(2,1)}, bf16[2048,8,128]{2,1,0:T(8,128)(2,1)}, u32[]{:S(2)}, u32[]{:S(2)}) collective-permute-start(bf16[2048,8,128]{2,1,0:T(8,128)(2,1)} %collective-permute-done.2.dy_ref), channel_id=1, source_target_pairs={{0,4},{4,0},{1,5},{5,1},{2,6},{6,2},{3,7},{7,3}} | collective-permute-start | bytes 12582920 | tf_op jit(solution)/shard_map/ppermute | solution.py:327
  224.3 91.8 %collective-permute-start.7 = (bf16[2048,8,128]{2,1,0:T(8,128)(2,1)}, bf16[2048,8,128]{2,1,0:T(8,128)(2,1)}, u32[]{:S(2)}, u32[]{:S(2)}) collective-permute-start(bf16[2048,8,128]{2,1,0:T(8,128)(2,1)} %collective-permute-done.6.x_ref), channel_id=1, source_target_pairs={{0,2},{1,3},{2,0},{3,1},{4,6},{5,7},{6,4},{7,5}} | collective-permute-start | bytes 12582920 | tf_op jit(solution)/shard_map/ppermute | solution.py:324
  281.3 94.6 %collective-permute-start.11 = (bf16[2048,8,128]{2,1,0:T(8,128)(2,1)}, bf16[2048,8,128]{2,1,0:T(8,128)(2,1)}, u32[]{:S(2)}, u32[]{:S(2)}) collective-permute-start(bf16[2048,8,128]{2,1,0:T(8,128)(2,1)} %collective-permute-done.6.x_ref), channel_id=1, source_target_pairs={{0,1},{1,0},{2,3},{3,2},{4,5},{5,4},{6,7},{7,6}} | collective-permute-start | bytes 12582920 | tf_op jit(solution)/shard_map/ppermute | solution.py:321
  282.4 93.5 %collective-permute-start.13 = (bf16[2048,8,128]{2,1,0:T(8,128)(2,1)}, bf16[2048,8,128]{2,1,0:T(8,128)(2,1)}, u32[]{:S(2)}, u32[]{:S(2)}) collective-permute-start(bf16[2048,8,128]{2,1,0:T(8,128)(2,1)} %collective-permute-done.12.dy_ref), channel_id=1, source_target_pairs={{0,1},{1,0},{2,3},{3,2},{4,5},{5,4},{6,7},{7,6}} | collective-permute-start | bytes 12582920 | tf_op jit(solution)/shard_map/ppermute | solution.py:321
  316.0 93.8 %collective-permute-start.8 = (bf16[2048,8,128]{2,1,0:T(8,128)(2,1)}, bf16[2048,8,128]{2,1,0:T(8,128)(2,1)}, u32[]{:S(2)}, u32[]{:S(2)}) collective-permute-start(bf16[2048,8,128]{2,1,0:T(8,128)(2,1)} %collective-permute-done.7.x_ref), channel_id=1, source_target_pairs={{0,1},{1,0},{2,3},{3,2},{4,5},{5,4},{6,7},{7,6}} | collective-permute-start | bytes 12582920 | tf_op jit(solution)/shard_map/ppermute | solution.py:321
  317.6 92.2 %collective-permute-start.10 = (bf16[2048,8,128]{2,1,0:T(8,128)(2,1)}, bf16[2048,8,128]{2,1,0:T(8,128)(2,1)}, u32[]{:S(2)}, u32[]{:S(2)}) collective-permute-start(bf16[2048,8,128]{2,1,0:T(8,128)(2,1)} %collective-permute-done.9.dy_ref), channel_id=1, source_target_pairs={{0,1},{1,0},{2,3},{3,2},{4,5},{5,4},{6,7},{7,6}} | collective-permute-start | bytes 12582920 | tf_op jit(solution)/shard_map/ppermute | solution.py:321
  579.1 393.7 %collective-permute-start.15 = (f32[2048,8,128]{2,1,0:T(8,128)}, f32[2048,8,128]{2,1,0:T(8,128)}, u32[]{:S(2)}, u32[]{:S(2)}) collective-permute-start(f32[2048,8,128]{2,1,0:T(8,128)} %combine.10), channel_id=1, source_target_pairs={{0,1},{1,0},{2,3},{3,2},{4,5},{5,4},{6,7},{7,6}} | collective-permute-start | bytes 25165832 | tf_op jit(solution)/shard_map/ppermute | solution.py:321
  602.0 400.2 %collective-permute-start.18 = (f32[2048,8,128]{2,1,0:T(8,128)}, f32[2048,8,128]{2,1,0:T(8,128)}, u32[]{:S(2)}, u32[]{:S(2)}) collective-permute-start(f32[2048,8,128]{2,1,0:T(8,128)} %combine.14), channel_id=1, source_target_pairs={{0,1},{1,0},{2,3},{3,2},{4,5},{5,4},{6,7},{7,6}} | collective-permute-start | bytes 25165832 | tf_op jit(solution)/shard_map/ppermute | solution.py:321
  602.1 363.0 %collective-permute-start.20 = (f32[2,1024,512]{2,1,0:T(8,128)}, f32[2,1024,512]{2,1,0:T(8,128)}, u32[]{:S(2)}, u32[]{:S(2)}) collective-permute-start(f32[2,1024,512]{2,1,0:T(8,128)} %get-tuple-element.137), channel_id=1, source_target_pairs={{0,4},{4,0},{1,5},{5,1},{2,6},{6,2},{3,7},{7,3}} | collective-permute-start | bytes 12582920 | tf_op jit(solution)/shard_map/ppermute | solution.py:327
  603.5 156.7 %collective-permute-start.24 = (f32[512,1024]{1,0:T(8,128)}, f32[512,1024]{1,0:T(8,128)}, u32[]{:S(2)}, u32[]{:S(2)}) collective-permute-start(f32[512,1024]{1,0:T(8,128)} %get-tuple-element.141), channel_id=1, source_target_pairs={{0,4},{4,0},{1,5},{5,1},{2,6},{6,2},{3,7},{7,3}} | collective-permute-start | bytes 6291464 | tf_op jit(solution)/shard_map/ppermute | solution.py:327
  603.5 193.0 %collective-permute-start.25 = (f32[512,1024]{1,0:T(8,128)}, f32[512,1024]{1,0:T(8,128)}, u32[]{:S(2)}, u32[]{:S(2)}) collective-permute-start(f32[512,1024]{1,0:T(8,128)} %get-tuple-element.142), channel_id=1, source_target_pairs={{0,4},{4,0},{1,5},{5,1},{2,6},{6,2},{3,7},{7,3}} | collective-permute-start | bytes 6291464 | tf_op jit(solution)/shard_map/ppermute | solution.py:327
  719.7 2.2 copy-start.7
  722.1 11.2 copy-start
  760.2 8.4 copy-start.9
  760.2 68.7 %collective-permute-start.26 = (f32[512,1024]{1,0:T(8,128)}, f32[512,1024]{1,0:T(8,128)}, u32[]{:S(2)}, u32[]{:S(2)}) collective-permute-start(f32[512,1024]{1,0:T(8,128)} %get-tuple-element.143), channel_id=1, source_target_pairs={{0,4},{4,0},{1,5},{5,1},{2,6},{6,2},{3,7},{7,3}} | collective-permute-start | bytes 6291464 | tf_op jit(solution)/shard_map/ppermute | solution.py:327
  796.5 205.5 %collective-permute-start.21 = (f32[2,1024,512]{2,1,0:T(8,128)}, f32[2,1024,512]{2,1,0:T(8,128)}, u32[]{:S(2)}, u32[]{:S(2)}) collective-permute-start(f32[2,1024,512]{2,1,0:T(8,128)} %get-tuple-element.138), channel_id=1, source_target_pairs={{0,4},{4,0},{1,5},{5,1},{2,6},{6,2},{3,7},{7,3}} | collective-permute-start | bytes 12582920 | tf_op jit(solution)/shard_map/ppermute | solution.py:327
  828.9 134.8 %collective-permute-start.27 = (f32[512,1024]{1,0:T(8,128)}, f32[512,1024]{1,0:T(8,128)}, u32[]{:S(2)}, u32[]{:S(2)}) collective-permute-start(f32[512,1024]{1,0:T(8,128)} %get-tuple-element.144), channel_id=1, source_target_pairs={{0,4},{4,0},{1,5},{5,1},{2,6},{6,2},{3,7},{7,3}} | collective-permute-start | bytes 6291464 | tf_op jit(solution)/shard_map/ppermute | solution.py:327
  963.7 188.3 %collective-permute-start.14 = (f32[2048,8,128]{2,1,0:T(8,128)}, f32[2048,8,128]{2,1,0:T(8,128)}, u32[]{:S(2)}, u32[]{:S(2)}) collective-permute-start(f32[2048,8,128]{2,1,0:T(8,128)} %combine.8), channel_id=1, source_target_pairs={{0,1},{1,0},{2,3},{3,2},{4,5},{5,4},{6,7},{7,6}} | collective-permute-start | bytes 25165832 | tf_op jit(solution)/shard_map/ppermute | solution.py:321
  965.0 92.4 %collective-permute-start.22 = (f32[2,1024,512]{2,1,0:T(8,128)}, f32[2,1024,512]{2,1,0:T(8,128)}, u32[]{:S(2)}, u32[]{:S(2)}) collective-permute-start(f32[2,1024,512]{2,1,0:T(8,128)} %get-tuple-element.139), channel_id=1, source_target_pairs={{0,4},{4,0},{1,5},{5,1},{2,6},{6,2},{3,7},{7,3}} | collective-permute-start | bytes 12582920 | tf_op jit(solution)/shard_map/ppermute | solution.py:327
  972.7 208.3 %collective-permute-start.17 = (f32[2048,8,128]{2,1,0:T(8,128)}, f32[2048,8,128]{2,1,0:T(8,128)}, u32[]{:S(2)}, u32[]{:S(2)}) collective-permute-start(f32[2048,8,128]{2,1,0:T(8,128)} %combine.12), channel_id=1, source_target_pairs={{0,1},{1,0},{2,3},{3,2},{4,5},{5,4},{6,7},{7,6}} | collective-permute-start | bytes 25165832 | tf_op jit(solution)/shard_map/ppermute | solution.py:321
  1002.1 145.3 %collective-permute-start.23 = (f32[2,1024,512]{2,1,0:T(8,128)}, f32[2,1024,512]{2,1,0:T(8,128)}, u32[]{:S(2)}, u32[]{:S(2)}) collective-permute-start(f32[2,1024,512]{2,1,0:T(8,128)} %get-tuple-element.140), channel_id=1, source_target_pairs={{0,4},{4,0},{1,5},{5,1},{2,6},{6,2},{3,7},{7,3}} | collective-permute-start | bytes 12582920 | tf_op jit(solution)/shard_map/ppermute | solution.py:327
  1002.2 204.5 %collective-permute-start.16 = (f32[2048,8,128]{2,1,0:T(8,128)}, f32[2048,8,128]{2,1,0:T(8,128)}, u32[]{:S(2)}, u32[]{:S(2)}) collective-permute-start(f32[2048,8,128]{2,1,0:T(8,128)} %combine.11), channel_id=1, source_target_pairs={{0,2},{1,3},{2,0},{3,1},{4,6},{5,7},{6,4},{7,5}} | collective-permute-start | bytes 25165832 | tf_op jit(solution)/shard_map/ppermute | solution.py:324
  1027.8 38.8 %copy-start.8 = (f32[512,1024]{1,0:T(8,128)S(1)}, f32[512,1024]{1,0:T(8,128)}, u32[]{:S(2)}) copy-start(f32[512,1024]{1,0:T(8,128)} %get-tuple-element.144) | copy-start | bytes 6291460
  1057.5 304.2 %collective-permute-start.19 = (f32[2048,8,128]{2,1,0:T(8,128)}, f32[2048,8,128]{2,1,0:T(8,128)}, u32[]{:S(2)}, u32[]{:S(2)}) collective-permute-start(f32[2048,8,128]{2,1,0:T(8,128)} %combine.15), channel_id=1, source_target_pairs={{0,2},{1,3},{2,0},{3,1},{4,6},{5,7},{6,4},{7,5}} | collective-permute-start | bytes 25165832 | tf_op jit(solution)/shard_map/ppermute | solution.py:324
  1066.6 9.8 copy-start.4
  1076.5 7.4 copy-start.6
  1083.9 7.4 copy-start.5
  1212.9 148.8 %copy-start.1 = (f32[2048,8,128]{2,1,0:T(8,128)S(1)}, f32[2048,8,128]{2,1,0:T(8,128)}, u32[]{:S(2)}) copy-start(f32[2048,8,128]{2,1,0:T(8,128)} %combine.13) | copy-start | bytes 25165828
Sparse Core Ops, SparseCore 0:
  27.3 51.2 all-reduce.2
